TPU v7x, 32 devices: a whole 2x2x4 slice. The times are simulated.
32 devices in a mesh: grp: 2 (over x), row: 16 (over z, y, core).
Axes of the slice: x: 2, y: 2, z: 4, core: 2. Of those that a mesh axis runs over, the one named last changes fastest.
Arguments:
- alignment: bfloat16 [128, 128, 256], P(('grp', 'row')), parts along dimension 0, may hold values from -6 to 6
- seq_flags: int32 [128], P(('grp', 'row')), parts along dimension 0, may hold values 0 or 1
- crop_flags: int32 [256], P('grp'), parts along dimension 0, may hold values 0 or 1
- norm_gain: float32 [256], replicated, may hold values from 0.5 to 1.5
- norm_bias: float32 [256], replicated, may hold values from -3 to 3
- left_weight: bfloat16 [256, 32], replicated, may hold values from -0.375 to 0.375
- left_bias: float32 [32], replicated, may hold values from -3 to 3
- right_weight: bfloat16 [256, 32], replicated, may hold values from -0.375 to 0.375
- right_bias: float32 [32], replicated, may hold values from -3 to 3
- out_weight: bfloat16 [1024, 128], replicated, may hold values from -0.1875 to 0.1875
- out_bias: float32 [128], replicated, may hold values from -3 to 3
Outputs:
- pair_update: bfloat16 [256, 128, 128], P(('grp', 'row')), parts along dimension 0
There are 2 independent parts, one for each index of `grp`. A program takes and returns all parts, laid end to end along the dimension named above; an argument that names none is the same for every part. Nothing has to cross between parts.
All inputs are finite; a program needn't handle non-finite values. No bound on the sum of `seq_flags` on one device may be relied on, other than what follows from the above.
Results may differ from a plain program's by a relative error of at most 0.004.
Values may be sent and summed in bfloat16 or wider, within the bound.
No kernel may reach another device: no remote copies, remote signals or barrier semaphores. Data moves between devices by JAX's collectives and lax.ppermute only.
A program may use at most 128 MiB of HBM per device.

v0:
```python
import jax
import jax.numpy as jnp
from jax import lax
from jax.sharding import PartitionSpec as P


def normalize(values, norm_gain, norm_bias):
    values = values.astype(jnp.float32)
    average = jnp.mean(values, axis=-1, keepdims=True)
    variance = jnp.mean((values - average) ** 2, axis=-1, keepdims=True)
    return (values - average) * lax.rsqrt(variance + 1e-05) * norm_gain + norm_bias


def project(normed, weight, bias, scaling):
    product = jnp.einsum(
        "src,cd->srd", normed, weight.astype(jnp.float32), precision=lax.Precision.HIGHEST
    )
    return ((product + bias) * scaling).astype(jnp.bfloat16)


def pair_tile(
    left_flat, column_piece, crop_rows, crop_cols, live_count, out_weight, out_bias, channels
):
    rows_here = crop_rows.shape[0]
    width_cols = column_piece.shape[1] // channels
    sums = lax.dot_general(
        left_flat, column_piece, (((0,), (0,)), ((), ())), preferred_element_type=jnp.float32
    )
    outer_sum = sums.reshape(rows_here, channels, width_cols, channels).transpose(0, 2, 1, 3)
    outer_sum = outer_sum.reshape(rows_here * width_cols, channels * channels).astype(jnp.bfloat16)
    projected = jnp.dot(outer_sum, out_weight, preferred_element_type=jnp.float32)
    projected = projected.reshape(rows_here, width_cols, out_weight.shape[1])
    divisor = jnp.maximum(live_count * crop_rows[:, None] * crop_cols[None, :], 1.0)
    return (projected / divisor[:, :, None] + out_bias).astype(jnp.bfloat16)


def column_blocks(
    left_flat, column_piece, crop_rows, crop_cols, live_count, out_weight, out_bias, channels
):
    rows_here = crop_rows.shape[0]
    width_cols = column_piece.shape[1] // channels
    span = max(1, 2048 // rows_here)
    if width_cols > span and width_cols % span == 0:

        def one_block(block_index):
            start = block_index * span
            piece_block = lax.dynamic_slice_in_dim(
                column_piece, start * channels, span * channels, 1
            )
            crop_block = lax.dynamic_slice_in_dim(crop_cols, start, span, 0)
            return pair_tile(
                left_flat,
                piece_block,
                crop_rows,
                crop_block,
                live_count,
                out_weight,
                out_bias,
                channels,
            )

        stacked = lax.map(one_block, jnp.arange(width_cols // span, dtype=jnp.int32))
        return stacked.transpose(1, 0, 2, 3).reshape(rows_here, width_cols, out_weight.shape[1])
    return pair_tile(
        left_flat, column_piece, crop_rows, crop_cols, live_count, out_weight, out_bias, channels
    )


def per_device(
    alignment,
    seq_flags,
    crop_flags,
    norm_gain,
    norm_bias,
    left_weight,
    left_bias,
    right_weight,
    right_bias,
    out_weight,
    out_bias,
):
    channels = left_weight.shape[1]
    devices_row = lax.axis_size("row")
    residues = alignment.shape[1]
    rows_here = residues // devices_row
    crop_float = crop_flags.astype(jnp.float32)
    my_index = lax.axis_index("row")
    crop_rows = lax.dynamic_slice_in_dim(crop_float, my_index * rows_here, rows_here, 0)
    regrouped = lax.all_to_all(alignment, "row", split_axis=1, concat_axis=0, tiled=True)
    all_flags = lax.all_gather(seq_flags, "row", axis=0, tiled=True)
    flag_float = all_flags.astype(jnp.float32)
    live_count = jnp.sum(flag_float)
    normed = normalize(regrouped, norm_gain, norm_bias)
    scaling = flag_float[:, None, None] * crop_rows[None, :, None]
    left = project(normed, left_weight, left_bias, scaling)
    right = project(normed, right_weight, right_bias, scaling)
    sequences = left.shape[0]
    left_flat = left.reshape(sequences, rows_here * channels)
    right_flat = right.reshape(sequences, rows_here * channels)
    return column_blocks(
        left_flat,
        lax.all_gather(right_flat, "row", axis=1, tiled=True),
        crop_rows,
        crop_float,
        live_count,
        out_weight,
        out_bias,
        channels,
    )


def solution(mesh):
    return jax.shard_map(
        per_device,
        mesh=mesh,
        in_specs=(
            P(("grp", "row"), None, None),
            P(("grp", "row")),
            P("grp"),
            P(),
            P(),
            P(),
            P(),
            P(),
            P(),
            P(),
            P(),
        ),
        out_specs=P(("grp", "row"), None, None),
        check_vma=False,
    )
```

profile of v0, /device:TPU:0, one launch (start us, length us, event | category | flops | bytes accessed | tf_op | source)
XLA Modules:
  0.0 54.4 jit_solution(9916558976857848131)
XLA Ops:
  0.0 0.0 copy-start
  0.0 0.0 copy-start.4
  0.0 0.0 copy-start.3
  0.0 1.9 %copy.75 = bf16[4,128,256]{2,0,1:T(4,128)(2,1)} copy(bf16[4,128,256]{2,1,0:T(8,128)(2,1)} %param.11) | data formatting | bytes 524288 | tf_op args[0]
  1.9 7.4 %all-to-all-start = ((bf16[4,128,256]{2,0,1:T(4,128)(2,1)}), bf16[4,128,256]{2,0,1:T(4,128)(2,1)S(1)}, u32[]{:S(2)}, u32[]{:S(2)}) async-start(bf16[4,128,256]{2,0,1:T(4,128)(2,1)} %copy.75), calls=%async_computation | async-start | bytes 524288 | tf_op jit(solution)/shard_map/all_to_all | solution.py:89
  9.3 0.0 copy-start.1
  9.3 0.0 copy-start.5
  9.4 1.3 %dynamic-slice = u32[1]{0:T(128)} dynamic-slice(u32[32]{0:T(128)} %constant.24, u32[]{:T(128)S(6)} %add.58), dynamic_slice_sizes={1} | dynamic-slice | bytes 12
  11.4 0.9 %dynamic-update-slice = s32[64]{0:T(128)S(1)} dynamic-update-slice(s32[64]{0:T(128)S(1)} %broadcast.80, s32[4]{0:T(128)} %param.12, u32[]{:T(128)} %bitcast.7) | dynamic-update-slice | bytes 36
  12.2 12.4 %all-reduce = s32[64]{0:T(128)S(1)} all-reduce(s32[64]{0:T(128)S(1)} %dynamic-update-slice), channel_id=1, replica_groups=mesh['grp'=2,'row'=16] {'row'}, use_global_device_ids=true, to_apply=%add | all-reduce | flops 64 | bytes 512
  24.7 0.7 %convert_reduce_fusion = f32[]{:T(128)} fusion(s32[64]{0:T(128)S(1)} %all-reduce), kind=kLoop, calls=%fused_computation.27 | loop fusion | flops 127 | bytes 260 | tf_op jit(solution)/shard_map/reduce_sum | solution.py:92
  25.4 0.7 %convert_element_type.51 = f32[128]{0:T(128)S(1)} convert(s32[128]{0:T(128)} %param.13) | non-fusion elementwise | flops 128 | bytes 1024 | tf_op jit(solution)/shard_map/convert_element_type | solution.py:86
  26.0 0.8 %broadcast_multiply_fusion.2 = (f32[8]{0:T(128)S(1)}, f32[8]{0:T(128)S(1)}) fusion(f32[]{:T(128)} %convert_reduce_fusion, f32[128]{0:T(128)S(1)} %convert_element_type.51, s32[]{:T(128)S(6)} %select_n.3), kind=kLoop, calls=%fused_computation.26 | loop fusion | flops 8 | bytes 104 | tf_op jit(solution)/shard_map/mul | solution.py:33
  26.8 0.1 multiply_maximum_fusion
  26.9 0.1 broadcast_multiply_fusion
  26.9 0.0 all-to-all-done
  26.9 0.1 fusion.10
  27.1 0.1 copy.79
  27.2 0.1 copy.81
  27.2 0.1 copy.80
  27.3 0.3 multiply_reduce_fusion
  27.6 0.1 copy.83
  27.7 0.1 copy.84
  27.9 0.0 copy-done.4
  27.9 0.0 copy-done.3
  27.9 0.0 copy-start.2
  27.9 0.0 copy-start.6
  27.9 0.2 fusion.9
  28.1 0.0 copy-done.1
  28.1 0.0 copy-done.5
  28.2 0.4 fusion.5
  28.5 0.1 copy.86
  28.7 21.0 %all_gather.7 = bf16[64,4096]{0,1:T(8,128)(2,1)S(1)} all-gather(bf16[64,256]{0,1:T(8,128)(2,1)S(1)} %bitcast.57), channel_id=1, replica_groups=mesh['grp'=2,'row'=16] {'row'}, dimensions={1}, use_global_device_ids=true | all-gather | bytes 557056 | tf_op jit(solution)/shard_map/all_gather | solution.py:102
  49.7 1.1 %copy.87 = bf16[128,32,64]{0,2,1:T(8,128)(2,1)S(1)} copy(bf16[128,32,64]{2,1,0:T(8,128)(2,1)S(1)} %bitcast.55) | data formatting | bytes 1048576 | tf_op jit(solution)/shard_map/dot_general | solution.py:26
  50.8 0.0 copy-done.2
  50.8 0.0 copy-done.6
  50.8 0.4 fusion.4
  51.2 0.1 copy.85
  51.3 0.7 %convert_bitcast_fusion = bf16[8,128,32,32]{1,2,3,0:T(8,128)(2,1)S(1)} fusion(bf16[128,32,64]{0,2,1:T(8,128)(2,1)S(1)} %copy.87, bf16[64,8,32]{0,2,1:T(8,128)(2,1)S(1)} %copy.85), kind=kOutput, calls=%fused_computation | convolution fusion | flops 135266304 | bytes 2654208 | tf_op jit(solution)/shard_map/dot_general | solution.py:26
  52.0 0.0 copy-start.7
  52.0 0.8 %copy.88 = bf16[8,128,32,32]{1,3,2,0:T(8,128)(2,1)S(1)} copy(bf16[8,128,32,32]{1,2,3,0:T(8,128)(2,1)S(1)} %convert_bitcast_fusion) | data formatting | bytes 4194304 | tf_op jit(solution)/shard_map/convert_element_type | solution.py:30
  52.9 0.0 copy-done
  52.9 0.0 copy-done.7
  52.9 1.5 %fusion.1 = bf16[8,128,128]{2,1,0:T(8,128)(2,1)} fusion(bf16[8,128,1024]{1,2,0:T(8,128)(2,1)S(1)} %bitcast.56, bf16[1024,128]{1,0:T(8,128)(2,1)S(1)} %copy-done, f32[128]{0:T(128)S(1)} %copy-done.7, f32[8,128]{1,0:T(8,128)S(1)} %multiply_maximum_fusion), kind=kOutput, calls=%fused_computation.3 | convolution fusion | flops 268828672 | bytes 2626048 | tf_op jit(solution)/shard_map/dot_general | solution.py:31
  (6 shorter events, 0.1 us)
Async XLA Ops:
  0.0 52.9 %copy-start = (bf16[1024,128]{1,0:T(8,128)(2,1)S(1)}, bf16[1024,128]{1,0:T(8,128)(2,1)}, u32[]{:S(2)}) copy-start(bf16[1024,128]{1,0:T(8,128)(2,1)} %param.20) | copy-start | bytes 786436
  0.0 27.9 %copy-start.4 = (f32[256]{0:T(256)S(1)}, f32[256]{0:T(256)}, u32[]{:S(2)}) copy-start(f32[256]{0:T(256)} %param.14) | copy-start | bytes 3076
  0.0 27.9 %copy-start.3 = (f32[256]{0:T(256)S(1)}, f32[256]{0:T(256)}, u32[]{:S(2)}) copy-start(f32[256]{0:T(256)} %param.15) | copy-start | bytes 3076
  1.9 25.0 %all-to-all-start = ((bf16[4,128,256]{2,0,1:T(4,128)(2,1)}), bf16[4,128,256]{2,0,1:T(4,128)(2,1)S(1)}, u32[]{:S(2)}, u32[]{:S(2)}) async-start(bf16[4,128,256]{2,0,1:T(4,128)(2,1)} %copy.75), calls=%async_computation | async-start | bytes 524288 | tf_op jit(solution)/shard_map/all_to_all | solution.py:89
  9.3 18.8 %copy-start.1 = (bf16[256,32]{0,1:T(8,128)(2,1)S(1)}, bf16[256,32]{0,1:T(8,128)(2,1)}, u32[]{:S(2)}) copy-start(bf16[256,32]{0,1:T(8,128)(2,1)} %param.18) | copy-start | bytes 49156
  9.3 18.8 %copy-start.5 = (f32[32]{0:T(128)S(1)}, f32[32]{0:T(128)}, u32[]{:S(2)}) copy-start(f32[32]{0:T(128)} %param.19) | copy-start | bytes 388
  27.9 22.9 %copy-start.2 = (bf16[256,32]{0,1:T(8,128)(2,1)S(1)}, bf16[256,32]{0,1:T(8,128)(2,1)}, u32[]{:S(2)}) copy-start(bf16[256,32]{0,1:T(8,128)(2,1)} %param.16) | copy-start | bytes 49156
  27.9 22.9 %copy-start.6 = (f32[32]{0:T(128)S(1)}, f32[32]{0:T(128)}, u32[]{:S(2)}) copy-start(f32[32]{0:T(128)} %param.17) | copy-start | bytes 388
  52.0 0.8 %copy-start.7 = (f32[128]{0:T(128)S(1)}, f32[128]{0:T(128)}, u32[]{:S(2)}) copy-start(f32[128]{0:T(128)} %param.21) | copy-start | bytes 1540
where the time goes:
time: 54.7 us; the launch traced here: 54.4 us
  blocking collectives  33.5 us (61%)
  starting transfers between devices  7.42 us (14%)
  local copies, waits for them, and re-layouts  6.75 us (12%)
  other arithmetic  2.94 us (5%)
  matrix products  2.91 us (5%)
  between operations  0.9 us (2%)
    all_gather x1, blocking collectives, per_device(): lax.all_gather(right_flat, 'row', axis=1, tiled=True)  21 us
    unnamed x1, blocking collectives  12.4 us
    all_to_all x1, starting transfers between devices, per_device(): lax.all_to_all(alignment, 'row', split_axis=1, concat_axis=0, tiled=True)  7.42 us
    unnamed x20, local copies, waits for them, and re-layouts  4.12 us
    dot_general x1, matrix products, pair_tile(): jnp.dot(outer_sum, out_weight, preferred_element_type=jnp.float32)  1.49 us
    dot_general x1, local copies, waits for them, and re-layouts, pair_tile(): lax.dot_general(left_flat, column_piece, (((0,), (0,)), ((), ())), prefer...  1.11 us
  transfers between devices with their start and end apart: 1, of which 0 were waited for; matrix products, arithmetic and copies ran while one was open for 8% of the time, Pallas kernels for 0%

commit v1 on v0

--- a/solution.py
+++ b/solution.py
@@ -2,6 +2,17 @@
 import jax.numpy as jnp
 from jax import lax
 from jax.sharding import PartitionSpec as P
+
+
+def cut_along(shard, dim, count):
+    before, after = (shard.shape[:dim], shard.shape[dim + 1 :])
+    return jnp.moveaxis(shard.reshape(*before, count, -1, *after), dim, 0)
+
+
+def joined_along(blocks, dim):
+    blocks = jnp.moveaxis(blocks, 0, dim)
+    shape = blocks.shape
+    return blocks.reshape(*shape[:dim], shape[dim] * shape[dim + 1], *shape[dim + 2 :])
 
 
 def normalize(values, norm_gain, norm_bias):
@@ -86,7 +97,14 @@
     crop_float = crop_flags.astype(jnp.float32)
     my_index = lax.axis_index("row")
     crop_rows = lax.dynamic_slice_in_dim(crop_float, my_index * rows_here, rows_here, 0)
-    regrouped = lax.all_to_all(alignment, "row", split_axis=1, concat_axis=0, tiled=True)
+    size, index = (lax.axis_size("row"), lax.axis_index("row"))
+    pieces = cut_along(alignment, 1, size)
+    outs = [pieces[index]]
+    for lap in range(1, size):
+        sent = pieces[index ^ lap]
+        outs.append(lax.ppermute(sent, "row", [(i, i ^ lap) for i in range(size)]))
+    pieces = jnp.stack(outs)[index ^ jnp.arange(size)]
+    regrouped = joined_along(pieces, 0)
     all_flags = lax.all_gather(seq_flags, "row", axis=0, tiled=True)
     flag_float = all_flags.astype(jnp.float32)
     live_count = jnp.sum(flag_float)

time: 54.7 us -> 74 us (1.35)
  starting transfers between devices: 7.42 us -> 20 us
  waiting for transfers between devices: 0.01 us -> 4.04 us
  blocking collectives: 33.5 us -> 36.3 us
    ppermute x0 -> x15, starting transfers between devices: none -> 20 us  [per_device(): outs.append(lax.ppermute(sent, 'row', [(i, i ^ lap) for i in range(size)]))]
    all_to_all x1 -> x0, starting transfers between devices: 7.42 us -> none  [per_device(): lax.all_to_all(alignment, 'row', split_axis=1, concat_axis=0, tiled=True)]
    ppermute x0 -> x15, waiting for transfers between devices: none -> 4.04 us  [per_device(): outs.append(lax.ppermute(sent, 'row', [(i, i ^ lap) for i in range(size)]))]
    all_gather x1, blocking collectives: 21 us -> 23.9 us  [per_device(): lax.all_gather(right_flat, 'row', axis=1, tiled=True)]
    unnamed x20 -> x34, local copies, waits for them, and re-layouts: 4.12 us -> 2.89 us
    squeeze x0 -> x1, local copies, waits for them, and re-layouts: none -> 0.97 us  [per_device(): sent = pieces[index ^ lap]]
  transfers between devices with their start and end apart: 1 -> 15, of which waited for: 0 -> 2; matrix products, arithmetic and copies ran while one was open for 8% -> 7% of each run, Pallas kernels for 0% -> 0%
where the time goes in v1:
time: 74 us; the launch traced here: 73.8 us
  blocking collectives  36.3 us (49%)
  starting transfers between devices  20 us (27%)
  local copies, waits for them, and re-layouts  6.62 us (9%)
  waiting for transfers between devices  4.04 us (5%)
  matrix products  2.91 us (4%)
  other arithmetic  2.82 us (4%)
  between operations  0.99 us (1%)
    all_gather x1, blocking collectives, per_device(): lax.all_gather(right_flat, 'row', axis=1, tiled=True)  23.9 us
    ppermute x15, starting transfers between devices, per_device(): outs.append(lax.ppermute(sent, 'row', [(i, i ^ lap) for i in range(size)]))  20 us
    unnamed x1, blocking collectives  12.4 us
    ppermute x15, waiting for transfers between devices, per_device(): outs.append(lax.ppermute(sent, 'row', [(i, i ^ lap) for i in range(size)]))  4.04 us
    unnamed x34, local copies, waits for them, and re-layouts  2.89 us
    dot_general x1, matrix products, pair_tile(): jnp.dot(outer_sum, out_weight, preferred_element_type=jnp.float32)  1.49 us
  transfers between devices with their start and end apart: 15, of which 2 were waited for; matrix products, arithmetic and copies ran while one was open for 7% of the time, Pallas kernels for 0%

profile of v1, /device:TPU:0, one launch (start us, length us, event | category | flops | bytes accessed | tf_op | source)
XLA Modules:
  0.0 73.8 jit_solution(9586829825203199771)
XLA Ops:
  0.1 1.0 %dynamic-slice_bitcast_fusion = (bf16[4,8,256]{2,1,0:T(8,128)(2,1)S(1)}, bf16[4,8,256]{2,1,0:T(8,128)(2,1)S(1)}, bf16[4,8,256]{2,1,0:T(8,128)(2,1)S(1)}, bf16[4,...) fusion(bf16[4,16,8,256]{3,2,1,0:T(8,128)(2,1)} %bitcast.113, ...), kind=kLoop, calls=%fused_computation.41 | loop fusion | bytes 491580 | tf_op jit(solution)/shard_map/squeeze | solution.py:104
  1.1 0.6 collective-permute-start
  1.6 2.6 %collective-permute-start.1 = (bf16[4,8,256]{2,1,0:T(8,128)(2,1)S(1)}, bf16[4,8,256]{2,1,0:T(8,128)(2,1)S(1)}, u32[]{:S(2)}, u32[]{:S(2)}) collective-permute-start(bf16[4,8,256]{2,1,0:T(8,128)(2,1)S(1)} %get-tuple-element.20), channel_id=1, source_target_pairs={{0,2},{1,3},{2,0},{3,1},{4,6},{5,7},{6,4},{7,5},{8,10},{9,11},{10,... | collective-permute-start | bytes 49160 | tf_op jit(solution)/shard_map/ppermute | solution.py:105
  4.2 0.0 collective-permute-start.2
  4.3 1.8 %collective-permute-start.3 = (bf16[4,8,256]{2,1,0:T(8,128)(2,1)S(1)}, bf16[4,8,256]{2,1,0:T(8,128)(2,1)S(1)}, u32[]{:S(2)}, u32[]{:S(2)}) collective-permute-start(bf16[4,8,256]{2,1,0:T(8,128)(2,1)S(1)} %get-tuple-element.18), channel_id=1, source_target_pairs={{0,4},{1,5},{2,6},{3,7},{4,0},{5,1},{6,2},{7,3},{8,12},{9,13},{10,... | collective-permute-start | bytes 49160 | tf_op jit(solution)/shard_map/ppermute | solution.py:105
  6.1 0.0 collective-permute-start.4
  6.1 1.2 %dynamic-slice.64 = u32[1]{0:T(128)} dynamic-slice(u32[32]{0:T(128)} %constant.56, u32[]{:T(128)S(6)} %add.133), dynamic_slice_sizes={1} | dynamic-slice | bytes 12
  8.0 0.9 %dynamic-update-slice = s32[64]{0:T(128)S(1)} dynamic-update-slice(s32[64]{0:T(128)S(1)} %broadcast.109, s32[4]{0:T(128)} %param.12, u32[]{:T(128)} %bitcast.37) | dynamic-update-slice | bytes 36
  8.8 12.4 %all-reduce = s32[64]{0:T(128)S(1)} all-reduce(s32[64]{0:T(128)S(1)} %dynamic-update-slice), channel_id=1, replica_groups=mesh['grp'=2,'row'=16] {'row'}, use_global_device_ids=true, to_apply=%add | all-reduce | flops 64 | bytes 512
  21.2 0.6 convert_reduce_fusion.1
  21.8 0.7 constant_dynamic-update-slice_fusion.15
  22.6 0.7 convert_element_type.41
  23.2 0.7 broadcast_multiply_fusion.2
  23.9 0.1 multiply_maximum_fusion
  24.0 0.1 broadcast_multiply_fusion
  24.1 0.0 collective-permute-done
  24.1 0.8 %collective-permute-start.5 = (bf16[4,8,256]{2,1,0:T(8,128)(2,1)S(1)}, bf16[4,8,256]{2,1,0:T(8,128)(2,1)S(1)}, u32[]{:S(2)}, u32[]{:S(2)}) collective-permute-start(bf16[4,8,256]{2,1,0:T(8,128)(2,1)S(1)} %get-tuple-element.16), channel_id=1, source_target_pairs={{0,6},{1,7},{2,4},{3,5},{4,2},{5,3},{6,0},{7,1},{8,14},{9,15},{10,... | collective-permute-start | bytes 49160 | tf_op jit(solution)/shard_map/ppermute | solution.py:105
  24.9 0.0 collective-permute-done.2
  25.0 0.4 collective-permute-start.7
  25.4 4.1 %collective-permute-start.8 = (bf16[4,8,256]{2,1,0:T(8,128)(2,1)S(1)}, bf16[4,8,256]{2,1,0:T(8,128)(2,1)S(1)}, u32[]{:S(2)}, u32[]{:S(2)}) collective-permute-start(bf16[4,8,256]{2,1,0:T(8,128)(2,1)S(1)} %get-tuple-element.13), channel_id=1, source_target_pairs={{0,9},{1,8},{2,11},{3,10},{4,13},{5,12},{6,15},{7,14},{8,1},{9,0},... | collective-permute-start | bytes 49160 | tf_op jit(solution)/shard_map/ppermute | solution.py:105
  29.5 0.0 collective-permute-done.4
  29.5 0.7 collective-permute-start.9
  30.2 1.1 %collective-permute-start.10 = (bf16[4,8,256]{2,1,0:T(8,128)(2,1)S(1)}, bf16[4,8,256]{2,1,0:T(8,128)(2,1)S(1)}, u32[]{:S(2)}, u32[]{:S(2)}) collective-permute-start(bf16[4,8,256]{2,1,0:T(8,128)(2,1)S(1)} %get-tuple-element.11), channel_id=1, source_target_pairs={{0,11},{1,10},{2,9},{3,8},{4,15},{5,14},{6,13},{7,12},{8,3},{9,2},... | collective-permute-start | bytes 49160 | tf_op jit(solution)/shard_map/ppermute | solution.py:105
  31.2 1.8 %collective-permute-start.11 = (bf16[4,8,256]{2,1,0:T(8,128)(2,1)S(1)}, bf16[4,8,256]{2,1,0:T(8,128)(2,1)S(1)}, u32[]{:S(2)}, u32[]{:S(2)}) collective-permute-start(bf16[4,8,256]{2,1,0:T(8,128)(2,1)S(1)} %get-tuple-element.10), channel_id=1, source_target_pairs={{0,12},{1,13},{2,14},{3,15},{4,8},{5,9},{6,10},{7,11},{8,4},{9,5},... | collective-permute-start | bytes 49160 | tf_op jit(solution)/shard_map/ppermute | solution.py:105
  33.0 3.6 %collective-permute-start.12 = (bf16[4,8,256]{2,1,0:T(8,128)(2,1)S(1)}, bf16[4,8,256]{2,1,0:T(8,128)(2,1)S(1)}, u32[]{:S(2)}, u32[]{:S(2)}) collective-permute-start(bf16[4,8,256]{2,1,0:T(8,128)(2,1)S(1)} %get-tuple-element.9), channel_id=1, source_target_pairs={{0,13},{1,12},{2,15},{3,14},{4,9},{5,8},{6,11},{7,10},{8,5},{9,4},... | collective-permute-start | bytes 49160 | tf_op jit(solution)/shard_map/ppermute | solution.py:105
  36.6 0.0 collective-permute-done.8
  36.6 0.7 collective-permute-start.13
  37.3 0.0 collective-permute-done.9
  37.3 2.0 %collective-permute-start.14 = (bf16[4,8,256]{2,1,0:T(8,128)(2,1)S(1)}, bf16[4,8,256]{2,1,0:T(8,128)(2,1)S(1)}, u32[]{:S(2)}, u32[]{:S(2)}) collective-permute-start(bf16[4,8,256]{2,1,0:T(8,128)(2,1)S(1)} %get-tuple-element.7), channel_id=1, source_target_pairs={{0,15},{1,14},{2,13},{3,12},{4,11},{5,10},{6,9},{7,8},{8,7},{9,6},... | collective-permute-start | bytes 49160 | tf_op jit(solution)/shard_map/ppermute | solution.py:105
  39.3 0.0 collective-permute-done.11
  39.3 3.8 %collective-permute-done.13 = bf16[4,8,256]{2,1,0:T(8,128)(2,1)S(1)} collective-permute-done((bf16[4,8,256]{2,1,0:T(8,128)(2,1)S(1)}, bf16[4,8,256]{2,1,0:T(8,128)(2,1)S(1)}, u32[]{:S(2)}, u32[]{:S(2)}) %collective-permute-start.13) | collective-permute-done | bytes 16416 | tf_op jit(solution)/shard_map/ppermute | solution.py:105
  43.1 0.2 collective-permute-done.14
  43.3 0.6 gather_fusion
  43.9 0.2 convert_reduce_fusion
  44.1 0.3 multiply_reduce_fusion
  44.4 0.0 copy-start.2
  44.4 0.0 copy-start.6
  44.4 0.2 fusion.9
  44.7 0.4 fusion.5
  45.0 0.1 copy.14
  45.2 23.9 %all_gather.7 = bf16[64,4096]{0,1:T(8,128)(2,1)S(1)} all-gather(bf16[64,256]{0,1:T(8,128)(2,1)S(1)} %bitcast.112), channel_id=1, replica_groups=mesh['grp'=2,'row'=16] {'row'}, dimensions={1}, use_global_device_ids=true | all-gather | bytes 557056 | tf_op jit(solution)/shard_map/all_gather | solution.py:120
  69.1 1.1 %copy.15 = bf16[128,32,64]{0,2,1:T(8,128)(2,1)S(1)} copy(bf16[128,32,64]{2,1,0:T(8,128)(2,1)S(1)} %bitcast.109) | data formatting | bytes 1048576 | tf_op jit(solution)/shard_map/dot_general | solution.py:37
  70.2 0.4 fusion.4
  70.6 0.1 copy.13
  70.7 0.7 convert_bitcast_fusion
  71.4 0.0 copy-start.7
  71.4 0.8 %copy.16 = bf16[8,128,32,32]{1,3,2,0:T(8,128)(2,1)S(1)} copy(bf16[8,128,32,32]{1,2,3,0:T(8,128)(2,1)S(1)} %convert_bitcast_fusion) | data formatting | bytes 4194304 | tf_op jit(solution)/shard_map/convert_element_type | solution.py:41
  72.3 1.5 %fusion.1 = bf16[8,128,128]{2,1,0:T(8,128)(2,1)} fusion(bf16[8,128,1024]{1,2,0:T(8,128)(2,1)S(1)} %bitcast.110, bf16[1024,128]{1,0:T(8,128)(2,1)S(1)} %copy-done, f32[128]{0:T(128)S(1)} %copy-done.7, f32[8,128]{1,0:T(8,128)S(1)} %multiply_maximum_fusion), kind=kOutput, calls=%fused_computation.4 | convolution fusion | flops 268828672 | bytes 2626048 | tf_op jit(solution)/shard_map/dot_general | solution.py:42
  (42 shorter events, 0.1 us)
Async XLA Ops:
  0.0 72.3 %copy-start = (bf16[1024,128]{1,0:T(8,128)(2,1)S(1)}, bf16[1024,128]{1,0:T(8,128)(2,1)}, u32[]{:S(2)}) copy-start(bf16[1024,128]{1,0:T(8,128)(2,1)} %param.20) | copy-start | bytes 786436
  0.0 44.4 %copy-start.4 = (f32[256]{0:T(256)S(1)}, f32[256]{0:T(256)}, u32[]{:S(2)}) copy-start(f32[256]{0:T(256)} %param.14) | copy-start | bytes 3076
  0.0 44.4 %copy-start.3 = (f32[256]{0:T(256)S(1)}, f32[256]{0:T(256)}, u32[]{:S(2)}) copy-start(f32[256]{0:T(256)} %param.15) | copy-start | bytes 3076
  0.0 44.6 %copy-start.1 = (bf16[256,32]{0,1:T(8,128)(2,1)S(1)}, bf16[256,32]{0,1:T(8,128)(2,1)}, u32[]{:S(2)}) copy-start(bf16[256,32]{0,1:T(8,128)(2,1)} %param.18) | copy-start | bytes 49156
  0.0 44.6 %copy-start.5 = (f32[32]{0:T(128)S(1)}, f32[32]{0:T(128)}, u32[]{:S(2)}) copy-start(f32[32]{0:T(128)} %param.19) | copy-start | bytes 388
  1.1 23.0 %collective-permute-start = (bf16[4,8,256]{2,1,0:T(8,128)(2,1)S(1)}, bf16[4,8,256]{2,1,0:T(8,128)(2,1)S(1)}, u32[]{:S(2)}, u32[]{:S(2)}) collective-permute-start(bf16[4,8,256]{2,1,0:T(8,128)(2,1)S(1)} %get-tuple-element.21), channel_id=1, source_target_pairs={{0,1},{1,0},{2,3},{3,2},{4,5},{5,4},{6,7},{7,6},{8,9},{9,8},{10,11... | collective-permute-start | bytes 49160 | tf_op jit(solution)/shard_map/ppermute | solution.py:105
  1.6 23.3 %collective-permute-start.1 = (bf16[4,8,256]{2,1,0:T(8,128)(2,1)S(1)}, bf16[4,8,256]{2,1,0:T(8,128)(2,1)S(1)}, u32[]{:S(2)}, u32[]{:S(2)}) collective-permute-start(bf16[4,8,256]{2,1,0:T(8,128)(2,1)S(1)} %get-tuple-element.20), channel_id=1, source_target_pairs={{0,2},{1,3},{2,0},{3,1},{4,6},{5,7},{6,4},{7,5},{8,10},{9,11},{10,... | collective-permute-start | bytes 49160 | tf_op jit(solution)/shard_map/ppermute | solution.py:105
  4.2 20.7 %collective-permute-start.2 = (bf16[4,8,256]{2,1,0:T(8,128)(2,1)S(1)}, bf16[4,8,256]{2,1,0:T(8,128)(2,1)S(1)}, u32[]{:S(2)}, u32[]{:S(2)}) collective-permute-start(bf16[4,8,256]{2,1,0:T(8,128)(2,1)S(1)} %get-tuple-element.19), channel_id=1, source_target_pairs={{0,3},{1,2},{2,1},{3,0},{4,7},{5,6},{6,5},{7,4},{8,11},{9,10},{10,... | collective-permute-start | bytes 49160 | tf_op jit(solution)/shard_map/ppermute | solution.py:105
  4.3 21.1 %collective-permute-start.3 = (bf16[4,8,256]{2,1,0:T(8,128)(2,1)S(1)}, bf16[4,8,256]{2,1,0:T(8,128)(2,1)S(1)}, u32[]{:S(2)}, u32[]{:S(2)}) collective-permute-start(bf16[4,8,256]{2,1,0:T(8,128)(2,1)S(1)} %get-tuple-element.18), channel_id=1, source_target_pairs={{0,4},{1,5},{2,6},{3,7},{4,0},{5,1},{6,2},{7,3},{8,12},{9,13},{10,... | collective-permute-start | bytes 49160 | tf_op jit(solution)/shard_map/ppermute | solution.py:105
  6.1 23.4 %collective-permute-start.4 = (bf16[4,8,256]{2,1,0:T(8,128)(2,1)S(1)}, bf16[4,8,256]{2,1,0:T(8,128)(2,1)S(1)}, u32[]{:S(2)}, u32[]{:S(2)}) collective-permute-start(bf16[4,8,256]{2,1,0:T(8,128)(2,1)S(1)} %get-tuple-element.17), channel_id=1, source_target_pairs={{0,5},{1,4},{2,7},{3,6},{4,1},{5,0},{6,3},{7,2},{8,13},{9,12},{10,... | collective-permute-start | bytes 49160 | tf_op jit(solution)/shard_map/ppermute | solution.py:105
  24.1 6.0 %collective-permute-start.5 = (bf16[4,8,256]{2,1,0:T(8,128)(2,1)S(1)}, bf16[4,8,256]{2,1,0:T(8,128)(2,1)S(1)}, u32[]{:S(2)}, u32[]{:S(2)}) collective-permute-start(bf16[4,8,256]{2,1,0:T(8,128)(2,1)S(1)} %get-tuple-element.16), channel_id=1, source_target_pairs={{0,6},{1,7},{2,4},{3,5},{4,2},{5,3},{6,0},{7,1},{8,14},{9,15},{10,... | collective-permute-start | bytes 49160 | tf_op jit(solution)/shard_map/ppermute | solution.py:105
  24.9 6.3 %collective-permute-start.6 = (bf16[4,8,256]{2,1,0:T(8,128)(2,1)S(1)}, bf16[4,8,256]{2,1,0:T(8,128)(2,1)S(1)}, u32[]{:S(2)}, u32[]{:S(2)}) collective-permute-start(bf16[4,8,256]{2,1,0:T(8,128)(2,1)S(1)} %get-tuple-element.15), channel_id=1, source_target_pairs={{0,7},{1,6},{2,5},{3,4},{4,3},{5,2},{6,1},{7,0},{8,15},{9,14},{10,... | collective-permute-start | bytes 49160 | tf_op jit(solution)/shard_map/ppermute | solution.py:105
  25.0 8.1 %collective-permute-start.7 = (bf16[4,8,256]{2,1,0:T(8,128)(2,1)S(1)}, bf16[4,8,256]{2,1,0:T(8,128)(2,1)S(1)}, u32[]{:S(2)}, u32[]{:S(2)}) collective-permute-start(bf16[4,8,256]{2,1,0:T(8,128)(2,1)S(1)} %get-tuple-element.14), channel_id=1, source_target_pairs={{0,8},{1,9},{2,10},{3,11},{4,12},{5,13},{6,14},{7,15},{8,0},{9,1},... | collective-permute-start | bytes 49160 | tf_op jit(solution)/shard_map/ppermute | solution.py:105
  25.4 11.2 %collective-permute-start.8 = (bf16[4,8,256]{2,1,0:T(8,128)(2,1)S(1)}, bf16[4,8,256]{2,1,0:T(8,128)(2,1)S(1)}, u32[]{:S(2)}, u32[]{:S(2)}) collective-permute-start(bf16[4,8,256]{2,1,0:T(8,128)(2,1)S(1)} %get-tuple-element.13), channel_id=1, source_target_pairs={{0,9},{1,8},{2,11},{3,10},{4,13},{5,12},{6,15},{7,14},{8,1},{9,0},... | collective-permute-start | bytes 49160 | tf_op jit(solution)/shard_map/ppermute | solution.py:105
  29.5 7.8 %collective-permute-start.9 = (bf16[4,8,256]{2,1,0:T(8,128)(2,1)S(1)}, bf16[4,8,256]{2,1,0:T(8,128)(2,1)S(1)}, u32[]{:S(2)}, u32[]{:S(2)}) collective-permute-start(bf16[4,8,256]{2,1,0:T(8,128)(2,1)S(1)} %get-tuple-element.12), channel_id=1, source_target_pairs={{0,10},{1,11},{2,8},{3,9},{4,14},{5,15},{6,12},{7,13},{8,2},{9,3},... | collective-permute-start | bytes 49160 | tf_op jit(solution)/shard_map/ppermute | solution.py:105
  30.2 9.1 %collective-permute-start.10 = (bf16[4,8,256]{2,1,0:T(8,128)(2,1)S(1)}, bf16[4,8,256]{2,1,0:T(8,128)(2,1)S(1)}, u32[]{:S(2)}, u32[]{:S(2)}) collective-permute-start(bf16[4,8,256]{2,1,0:T(8,128)(2,1)S(1)} %get-tuple-element.11), channel_id=1, source_target_pairs={{0,11},{1,10},{2,9},{3,8},{4,15},{5,14},{6,13},{7,12},{8,3},{9,2},... | collective-permute-start | bytes 49160 | tf_op jit(solution)/shard_map/ppermute | solution.py:105
  31.2 8.0 %collective-permute-start.11 = (bf16[4,8,256]{2,1,0:T(8,128)(2,1)S(1)}, bf16[4,8,256]{2,1,0:T(8,128)(2,1)S(1)}, u32[]{:S(2)}, u32[]{:S(2)}) collective-permute-start(bf16[4,8,256]{2,1,0:T(8,128)(2,1)S(1)} %get-tuple-element.10), channel_id=1, source_target_pairs={{0,12},{1,13},{2,14},{3,15},{4,8},{5,9},{6,10},{7,11},{8,4},{9,5},... | collective-permute-start | bytes 49160 | tf_op jit(solution)/shard_map/ppermute | solution.py:105
  33.0 6.2 %collective-permute-start.12 = (bf16[4,8,256]{2,1,0:T(8,128)(2,1)S(1)}, bf16[4,8,256]{2,1,0:T(8,128)(2,1)S(1)}, u32[]{:S(2)}, u32[]{:S(2)}) collective-permute-start(bf16[4,8,256]{2,1,0:T(8,128)(2,1)S(1)} %get-tuple-element.9), channel_id=1, source_target_pairs={{0,13},{1,12},{2,15},{3,14},{4,9},{5,8},{6,11},{7,10},{8,5},{9,4},... | collective-permute-start | bytes 49160 | tf_op jit(solution)/shard_map/ppermute | solution.py:105
  36.6 6.5 %collective-permute-start.13 = (bf16[4,8,256]{2,1,0:T(8,128)(2,1)S(1)}, bf16[4,8,256]{2,1,0:T(8,128)(2,1)S(1)}, u32[]{:S(2)}, u32[]{:S(2)}) collective-permute-start(bf16[4,8,256]{2,1,0:T(8,128)(2,1)S(1)} %get-tuple-element.8), channel_id=1, source_target_pairs={{0,14},{1,15},{2,12},{3,13},{4,10},{5,11},{6,8},{7,9},{8,6},{9,7},... | collective-permute-start | bytes 49160 | tf_op jit(solution)/shard_map/ppermute | solution.py:105
  37.3 6.0 %collective-permute-start.14 = (bf16[4,8,256]{2,1,0:T(8,128)(2,1)S(1)}, bf16[4,8,256]{2,1,0:T(8,128)(2,1)S(1)}, u32[]{:S(2)}, u32[]{:S(2)}) collective-permute-start(bf16[4,8,256]{2,1,0:T(8,128)(2,1)S(1)} %get-tuple-element.7), channel_id=1, source_target_pairs={{0,15},{1,14},{2,13},{3,12},{4,11},{5,10},{6,9},{7,8},{8,7},{9,6},... | collective-permute-start | bytes 49160 | tf_op jit(solution)/shard_map/ppermute | solution.py:105
  44.4 25.8 %copy-start.2 = (bf16[256,32]{0,1:T(8,128)(2,1)S(1)}, bf16[256,32]{0,1:T(8,128)(2,1)}, u32[]{:S(2)}) copy-start(bf16[256,32]{0,1:T(8,128)(2,1)} %param.16) | copy-start | bytes 49156
  44.4 25.8 %copy-start.6 = (f32[32]{0:T(128)S(1)}, f32[32]{0:T(128)}, u32[]{:S(2)}) copy-start(f32[32]{0:T(128)} %param.17) | copy-start | bytes 388
  71.4 0.8 %copy-start.7 = (f32[128]{0:T(128)S(1)}, f32[128]{0:T(128)}, u32[]{:S(2)}) copy-start(f32[128]{0:T(128)} %param.21) | copy-start | bytes 1540
